TPU v7x, 32 devices: a whole 2x2x4 slice. The times are simulated.
32 devices in a mesh: groups: 2 (over x), expert: 8 (over z, y), dp: 2 (over core).
Axes of the slice: x: 2, y: 2, z: 4, core: 2. Of those that a mesh axis runs over, the one named last changes fastest.
Arguments:
- tokens: bfloat16 [128, 2880], P(('groups', 'expert', 'dp')), parts along dimension 0, may hold values from -6 to 6
- norm_gain: bfloat16 [2, 2880], replicated, may hold values from 0.25 to 1.75
- w_gate: bfloat16 [2, 2880, 23040], P(None, None, ('expert', 'dp')), may hold values from -0.109375 to 0.109375
- w_up: bfloat16 [2, 2880, 23040], P(None, None, ('expert', 'dp')), may hold values from -0.109375 to 0.109375
- w_down: bfloat16 [2, 23040, 2880], P(None, ('expert', 'dp')), may hold values from -0.109375 to 0.109375
- routes: int32 [2, 128, 4], P(None, ('groups', 'expert', 'dp')), parts along dimension 1, may hold values from 0 to 7, all different within a row; in each aligned block of 4 rows (0 to 3, 4 to 7, ..., all dimensions but the last counted through in order) at most 3 rows name the same one
- gates: float32 [2, 128, 4], P(None, ('groups', 'expert', 'dp')), parts along dimension 1, may hold values from 0.1 to 1
Outputs:
- mixed: bfloat16 [128, 2880], P(('groups', 'expert', 'dp')), parts along dimension 0
There are 2 independent parts, one for each index of `groups`. A program takes and returns all parts, laid end to end along the dimension named above; an argument that names none is the same for every part. Nothing has to cross between parts.
Inputs may be any that keep to these rules, and one draw needn't show every extreme that they name: `routes`: each token names 4 different experts; among the 4 rows of one device (aligned blocks of a layer) no expert is named more than 3 times, and in every layer some device's block names some expert exactly 3 times.
All inputs are finite; a program needn't handle non-finite values.
Results may differ from a plain program's by a relative error of at most 0.014.
Values may be sent and summed in bfloat16 or wider, within the bound.
No kernel may reach another device: no remote copies, remote signals or barrier semaphores. Data moves between devices by JAX's collectives and lax.ppermute only.
A program may use at most 128 MiB of HBM per device.

v0:
```python
import jax
import jax.numpy as jnp
from jax import lax
from jax.sharding import PartitionSpec as P

D = 2880
FF = 2880
LAYERS = 2
CAP = 3


def expert_rows(inputs, gate_cols, up_cols, down_rows):
    leading = inputs.shape[:-1]
    flat_rows = inputs.reshape(-1, inputs.shape[-1])
    gate_val = jnp.dot(flat_rows, gate_cols, preferred_element_type=jnp.float32)
    up_val = jnp.dot(flat_rows, up_cols, preferred_element_type=jnp.float32)
    active = (gate_val * jax.nn.sigmoid(1.702 * gate_val) * (up_val + 1.0)).astype(jnp.bfloat16)
    result = jnp.dot(active, down_rows, preferred_element_type=jnp.float32)
    return result.reshape(leading + (down_rows.shape[1],))


def on_device(tokens, norm_gain, w_gate, w_up, w_down, routes, gates):
    token_count = tokens.shape[0]
    top_count = routes.shape[2]
    expert_size = lax.axis_size("expert")
    pair_size = lax.axis_size("dp")
    device_count = expert_size * pair_size
    expert_total = device_count * w_down.shape[1] // FF
    shard_count = device_count // expert_total
    slot_count = CAP
    hidden_state = tokens
    for layer_idx in range(LAYERS):
        widened = hidden_state.astype(jnp.float32)
        scale_inv = lax.rsqrt(jnp.mean(widened * widened, axis=-1, keepdims=True) + 1e-05)
        normed = (widened * scale_inv * norm_gain[layer_idx].astype(jnp.float32)).astype(
            jnp.bfloat16
        )
        expert_ids = routes[layer_idx].reshape(token_count * top_count)
        one_hot = (
            expert_ids[:, None] == jnp.arange(expert_total, dtype=jnp.int32)[None, :]
        ).astype(jnp.int32)
        slot_index = jnp.sum((jnp.cumsum(one_hot, axis=0) - one_hot) * one_hot, axis=1)
        column = expert_ids * slot_count + slot_index
        placed = column[:, None] == jnp.arange(expert_total * slot_count, dtype=jnp.int32)[None, :]
        placed_f = placed.astype(jnp.float32).reshape(
            token_count, top_count, expert_total * slot_count
        )
        combine_mat = jnp.sum(placed_f * gates[layer_idx][:, :, None], axis=1)
        pack_mat = jnp.sum(placed_f, axis=1).T.astype(jnp.bfloat16)
        packed = jnp.dot(pack_mat, normed, preferred_element_type=jnp.float32).astype(jnp.bfloat16)
        packed = packed.reshape(expert_total, slot_count, D)
        gate_cols = w_gate[layer_idx]
        up_cols = w_up[layer_idx]
        down_rows = w_down[layer_idx]
        outgoing = jnp.repeat(packed, shard_count // pair_size, axis=0)
        arrived = lax.all_to_all(outgoing, "expert", split_axis=0, concat_axis=0, tiled=True)
        paired = lax.all_gather(arrived[:, None], "dp", axis=1, tiled=True)
        partial_value = expert_rows(
            paired.reshape(device_count, slot_count, D), gate_cols, up_cols, down_rows
        )
        returned = lax.all_to_all(
            partial_value, ("expert", "dp"), split_axis=0, concat_axis=0, tiled=True
        )
        summed = jnp.sum(returned.reshape(expert_total, shard_count, slot_count, D), axis=1)
        mixture = jnp.dot(
            combine_mat,
            summed.reshape(expert_total * slot_count, D),
            precision=lax.Precision.HIGHEST,
        )
        hidden_state = (widened + mixture).astype(jnp.bfloat16)
    return hidden_state


def solution(mesh):
    return jax.shard_map(
        on_device,
        mesh=mesh,
        in_specs=(
            P(("groups", "expert", "dp"), None),
            P(),
            P(None, None, ("expert", "dp")),
            P(None, None, ("expert", "dp")),
            P(None, ("expert", "dp"), None),
            P(None, ("groups", "expert", "dp"), None),
            P(None, ("groups", "expert", "dp"), None),
        ),
        out_specs=P(("groups", "expert", "dp"), None),
        check_vma=False,
    )
```

profile of v0, /device:TPU:0, one launch (start us, length us, event | category | flops | bytes accessed | tf_op | source)
XLA Modules:
  0.0 118.9 jit_solution(5471143128562517334)
XLA Ops:
  0.0 0.9 fusion.41
  0.9 0.7 slice_bitcast_fusion
  1.6 0.7 fusion.53
  2.3 0.1 eq.65
  2.4 0.1 eq.58
  2.5 0.1 fusion.50
  2.6 0.2 select_reduce_fusion.3
  2.8 0.1 reduce_sum.95
  2.8 0.1 fusion.49
  2.9 0.2 select_reduce_fusion.1
  3.1 0.1 reduce_sum.101
  3.2 0.9 convert_reduce_fusion
  4.1 0.7 bitcast_add_fusion
  4.8 0.1 convert_reduce_fusion.2
  4.9 1.0 convolution_convert_fusion.1
  5.9 0.1 reshape_broadcast_in_dim_reshape.6
  6.0 14.9 %all_to_all.20 = bf16[8,3,2880]{2,1,0:T(4,128)(2,1)S(1)} all-to-all(bf16[8,3,2880]{2,1,0:T(4,128)(2,1)S(1)} %reshape_broadcast_in_dim_reshape.6), channel_id=1, replica_groups=mesh['groups'=2,'expert'=8,'dp'=2] {'expert'}, dimensions={0} | all-to-all | bytes 276480 | tf_op jit(solution)/shard_map/all_to_all | solution.py:56
  20.9 2.0 %all-gather = bf16[8,6,2880]{2,0,1:T(8,128)(2,1)S(1)} all-gather(bf16[8,3,2880]{2,0,1:T(8,128)(2,1)S(1)} %copy.24), channel_id=2, replica_groups=mesh['groups'=2,'expert'=8,'dp'=2] {'dp'}, dimensions={1}, use_global_device_ids=true | all-gather | bytes 414720 | tf_op jit(solution)/shard_map/all_gather | solution.py:57
  23.0 0.2 reshape_reshape.6
  23.1 0.0 copy-start
  23.2 5.9 %fusion.10 = f32[48,1440]{1,0:T(8,128)S(1)} fusion(bf16[48,2880]{1,0:T(8,128)(2,1)S(1)} %reshape_reshape.6, bf16[2,2880,1440]{1,2,0:T(8,128)(2,1)} %param.9), kind=kOutput, calls=%fused_computation.10 | convolution fusion | flops 398131200 | bytes 9031680 | tf_op jit(solution)/shard_map/dot_general | solution.py:15
  29.1 5.9 %fusion.36 = bf16[48,1440]{1,0:T(8,128)(2,1)S(1)} fusion(bf16[48,2880]{1,0:T(8,128)(2,1)S(1)} %reshape_reshape.6, bf16[2,2880,1440]{1,2,0:T(8,128)(2,1)} %param.10, f32[48,1440]{1,0:T(8,128)S(1)} %fusion.10), kind=kOutput, calls=%fused_computation.30 | convolution fusion | flops 398684160 | bytes 9169920 | tf_op jit(solution)/shard_map/dot_general | solution.py:16
  35.0 0.1 dot_general.37
  35.1 4.9 %fusion.6 = f32[16,3,2880]{2,0,1:T(8,128)S(1)} fusion(bf16[2,1440,2880]{2,1,0:T(8,128)(2,1)} %param.11, bf16[16,3,1440]{2,1,0:T(4,128)(2,1)S(1)} %dot_general.37), kind=kOutput, calls=%fused_computation.6 | convolution fusion | flops 398131200 | bytes 9169920 | tf_op jit(solution)/shard_map/dot_general | solution.py:18
  40.0 0.3 copy.27
  40.3 22.6 %all_to_all.21 = f32[16,3,2880]{2,1,0:T(4,128)S(1)} all-to-all(f32[16,3,2880]{2,1,0:T(4,128)S(1)} %copy.27), channel_id=1, replica_groups=mesh['groups'=2,'expert'=8,'dp'=2] {'expert','dp'}, dimensions={0} | all-to-all | bytes 1105920 | tf_op jit(solution)/shard_map/all_to_all | solution.py:61
  62.8 0.1 bitcast_reduce_fusion.1
  63.0 0.1 reshape.77
  63.1 0.0 copy-done
  63.1 0.4 multiply_reduce_fusion
  63.5 0.3 convolution_convert_fusion
  63.8 0.1 reshape_broadcast_in_dim_reshape.7
  63.9 11.9 %all_to_all.22 = bf16[8,3,2880]{2,1,0:T(4,128)(2,1)S(1)} all-to-all(bf16[8,3,2880]{2,1,0:T(4,128)(2,1)S(1)} %reshape_broadcast_in_dim_reshape.7), channel_id=1, replica_groups=mesh['groups'=2,'expert'=8,'dp'=2] {'expert'}, dimensions={0} | all-to-all | bytes 276480 | tf_op jit(solution)/shard_map/all_to_all | solution.py:56
  75.8 2.0 %all-gather.1 = bf16[8,6,2880]{2,0,1:T(8,128)(2,1)S(1)} all-gather(bf16[8,3,2880]{2,0,1:T(8,128)(2,1)S(1)} %copy.30), channel_id=3, replica_groups=mesh['groups'=2,'expert'=8,'dp'=2] {'dp'}, dimensions={1}, use_global_device_ids=true | all-gather | bytes 414720 | tf_op jit(solution)/shard_map/all_gather | solution.py:57
  77.8 0.2 reshape_reshape.7
  78.0 5.9 %fusion.4 = f32[48,1440]{1,0:T(8,128)S(1)} fusion(bf16[48,2880]{1,0:T(8,128)(2,1)S(1)} %reshape_reshape.7, bf16[2,2880,1440]{1,2,0:T(8,128)(2,1)} %param.9), kind=kOutput, calls=%fused_computation.4 | convolution fusion | flops 398131200 | bytes 9031680 | tf_op jit(solution)/shard_map/dot_general | solution.py:15
  83.9 5.9 %fusion.33 = bf16[48,1440]{1,0:T(8,128)(2,1)S(1)} fusion(bf16[48,2880]{1,0:T(8,128)(2,1)S(1)} %reshape_reshape.7, bf16[2,2880,1440]{1,2,0:T(8,128)(2,1)} %param.10, f32[48,1440]{1,0:T(8,128)S(1)} %fusion.4), kind=kOutput, calls=%fused_computation.29 | convolution fusion | flops 398684160 | bytes 9169920 | tf_op jit(solution)/shard_map/dot_general | solution.py:16
  89.9 0.1 dot_general.43
  89.9 4.9 %fusion = f32[16,3,2880]{2,0,1:T(8,128)S(1)} fusion(bf16[2,1440,2880]{2,1,0:T(8,128)(2,1)} %param.11, bf16[16,3,1440]{2,1,0:T(4,128)(2,1)S(1)} %dot_general.43), kind=kOutput, calls=%fused_computation | convolution fusion | flops 398131200 | bytes 9169920 | tf_op jit(solution)/shard_map/dot_general | solution.py:18
  94.8 0.3 copy.33
  95.1 22.5 %all_to_all.23 = f32[16,3,2880]{2,1,0:T(4,128)S(1)} all-to-all(f32[16,3,2880]{2,1,0:T(4,128)S(1)} %copy.33), channel_id=1, replica_groups=mesh['groups'=2,'expert'=8,'dp'=2] {'expert','dp'}, dimensions={0} | all-to-all | bytes 1105920 | tf_op jit(solution)/shard_map/all_to_all | solution.py:61
  117.7 0.1 bitcast_reduce_fusion
  117.8 0.1 reshape.79
  118.0 0.9 fusion.19
  (8 shorter events, 0.2 us)
Async XLA Ops:
  23.1 40.0 %copy-start = (bf16[4,2880]{1,0:T(4,128)(2,1)S(1)}, bf16[4,2880]{1,0:T(4,128)(2,1)}, u32[]{:S(2)}) copy-start(bf16[4,2880]{1,0:T(4,128)(2,1)} %param.7) | copy-start | bytes 69124
where the time goes:
time: 120 us; the launch traced here: 119 us
  blocking collectives  75.9 us (63%)
  matrix products  35.9 us (30%)
  other arithmetic  3.45 us (3%)
  local copies, waits for them, and re-layouts  3.41 us (3%)
    all_to_all x2, blocking collectives, on_device(): lax.all_to_all(partial_value, ('expert', 'dp'), split_axis=0, concat_axis...  45.1 us
    all_to_all x2, blocking collectives, on_device(): lax.all_to_all(outgoing, 'expert', split_axis=0, concat_axis=0, tiled=True)  26.8 us
    dot_general x2, matrix products, expert_rows(): gate_val = jnp.dot(flat_rows, gate_cols, preferred_element_type=jnp.float32)  11.8 us
    dot_general x2, matrix products, expert_rows(): up_val = jnp.dot(flat_rows, up_cols, preferred_element_type=jnp.float32)  11.8 us
    dot_general x2, matrix products, expert_rows(): result = jnp.dot(active, down_rows, preferred_element_type=jnp.float32)  9.75 us
    all_gather x2, blocking collectives, on_device(): paired = lax.all_gather(arrived[:, None], 'dp', axis=1, tiled=True)  4.02 us

commit v1 on v0

v1 whole, which is shorter than its diff:
```python
import functools

import jax
import jax.numpy as jnp
from jax import lax
from jax.experimental import pallas as pl
from jax.experimental.pallas import tpu as pltpu
from jax.sharding import PartitionSpec as P

EPS = 1e-05
VMEM_LIMIT = 20 * 1024 * 1024


def normalise(value, gain_row):
    scale_inv = lax.rsqrt(jnp.mean(value * value, axis=-1, keepdims=True) + EPS)
    return (value * scale_inv * gain_row.astype(jnp.float32)).astype(jnp.bfloat16)


def first_norm_kernel(tokens_ref, gain_ref, normed_ref):
    normed_ref[...] = normalise(tokens_ref[...].astype(jnp.float32), gain_ref[0:1, :])


def first_norm(tokens, norm_gain):
    return pl.pallas_call(
        first_norm_kernel,
        out_shape=jax.ShapeDtypeStruct(tokens.shape, jnp.bfloat16),
        name="first_norm",
    )(tokens, norm_gain)


def hidden_block(hidden):
    for block in (240, 480, 288, 144, 96, 720):
        if hidden % block == 0:
            return block
    return hidden


def experts_kernel(mine_ref, other_ref, gate_ref, up_ref, down_ref, keep_ref, send_ref, rows_ref, acc_ref):
    step = pl.program_id(0)
    half = mine_ref.shape[0]

    @pl.when(step == 0)
    def _():
        rows_ref[:half, :] = mine_ref[...]
        rows_ref[half:, :] = other_ref[...]

    rows = rows_ref[...]
    across = (((1,), (1,)), ((), ()))
    gate_val = lax.dot_general(rows, gate_ref[0], across, preferred_element_type=jnp.float32)
    up_val = lax.dot_general(rows, up_ref[0], across, preferred_element_type=jnp.float32)
    active = (gate_val * jax.nn.sigmoid(1.702 * gate_val) * (up_val + 1.0)).astype(jnp.bfloat16)
    part = jnp.dot(active, down_ref[0], preferred_element_type=jnp.float32)

    @pl.when(step == 0)
    def _():
        acc_ref[...] = part

    @pl.when(step > 0)
    def _():
        acc_ref[...] += part

    @pl.when(step == pl.num_programs(0) - 1)
    def _():
        keep_ref[...] = acc_ref[:half, :].astype(jnp.bfloat16)
        send_ref[...] = acc_ref[half:, :].astype(jnp.bfloat16)


def experts(layer_idx, mine, other, gate_rows, up_rows, down_rows):
    half, width = mine.shape
    hidden = down_rows.shape[1]
    block = hidden_block(hidden)
    whole = pl.BlockSpec((half, width), lambda i: (0, 0))
    weight = pl.BlockSpec((1, block, width), lambda i: (layer_idx, i, 0))
    return pl.pallas_call(
        experts_kernel,
        grid=(hidden // block,),
        in_specs=[whole, whole, weight, weight, weight],
        out_specs=[whole, whole],
        out_shape=[jax.ShapeDtypeStruct((half, width), jnp.bfloat16)] * 2,
        scratch_shapes=[
            pltpu.VMEM((2 * half, width), jnp.bfloat16),
            pltpu.VMEM((2 * half, width), jnp.float32),
        ],
        compiler_params=pltpu.CompilerParams(vmem_limit_bytes=VMEM_LIMIT),
        name="experts",
    )(mine, other, gate_rows, up_rows, down_rows)


def combine_kernel(layer_idx, chips_per_expert, last, state_ref, parts_ref, routes_ref, gates_ref, gain_ref, *out_refs):
    routes = routes_ref[layer_idx]
    gates = gates_ref[layer_idx]
    total = jnp.zeros(state_ref.shape, jnp.float32)
    for chip in range(parts_ref.shape[0]):
        weight = jnp.sum(jnp.where(routes == chip // chips_per_expert, gates, 0.0), axis=1, keepdims=True)
        total = total + weight * parts_ref[chip].astype(jnp.float32)
    state = (state_ref[...].astype(jnp.float32) + total).astype(jnp.bfloat16)
    out_refs[0][...] = state
    if not last:
        out_refs[1][...] = normalise(state.astype(jnp.float32), gain_ref[layer_idx + 1 : layer_idx + 2, :])


def combine(layer_idx, last, chips_per_expert, state, parts, routes, gates, norm_gain):
    shape = jax.ShapeDtypeStruct(state.shape, jnp.bfloat16)
    return pl.pallas_call(
        functools.partial(combine_kernel, layer_idx, chips_per_expert, last),
        out_shape=[shape] if last else [shape, shape],
        compiler_params=pltpu.CompilerParams(vmem_limit_bytes=VMEM_LIMIT),
        name="combine",
    )(state, parts, routes, gates, norm_gain)


def on_device(tokens, norm_gain, w_gate, w_up, w_down, routes, gates):
    token_count, width = tokens.shape
    layers = norm_gain.shape[0]
    chips = lax.axis_size("expert")
    pair_size = lax.axis_size("dp")
    expert_total = chips * pair_size * w_down.shape[1] // width
    chips_per_expert = chips // expert_total
    swap = [(0, 1), (1, 0)]
    gate_rows = jnp.swapaxes(w_gate, 1, 2)
    up_rows = jnp.swapaxes(w_up, 1, 2)
    state = tokens
    normed = first_norm(tokens, norm_gain)
    for layer_idx in range(layers):
        outgoing = jnp.broadcast_to(normed[None], (chips, token_count, width))
        arrived = lax.all_to_all(outgoing, "expert", split_axis=0, concat_axis=0, tiled=True)
        mine = arrived.reshape(chips * token_count, width)
        other = lax.ppermute(mine, "dp", swap)
        keep, send = experts(layer_idx, mine, other, gate_rows, up_rows, w_down)
        got = lax.ppermute(send, "dp", swap)
        paired = (keep + got).reshape(chips, token_count, width)
        parts = lax.all_to_all(paired, "expert", split_axis=0, concat_axis=0, tiled=True)
        last = layer_idx == layers - 1
        results = combine(layer_idx, last, chips_per_expert, state, parts, routes, gates, norm_gain)
        state = results[0]
        normed = results[-1]
    return state


def solution(mesh):
    return jax.shard_map(
        on_device,
        mesh=mesh,
        in_specs=(
            P(("groups", "expert", "dp"), None),
            P(),
            P(None, None, ("expert", "dp")),
            P(None, None, ("expert", "dp")),
            P(None, ("expert", "dp"), None),
            P(None, ("groups", "expert", "dp"), None),
            P(None, ("groups", "expert", "dp"), None),
        ),
        out_specs=P(("groups", "expert", "dp"), None),
        check_vma=False,
    )
```

time: 120 us -> 101 us (0.84)
  matrix products: 35.9 us -> 0 us
  blocking collectives: 75.9 us -> 47.5 us
  Pallas kernels: 0 us -> 22.7 us
  local copies, waits for them, and re-layouts: 3.41 us -> 24.4 us
  waiting for transfers between devices: 0 us -> 5.41 us
  other arithmetic: 3.45 us -> 0.1 us
    dot_general x10 -> x0, matrix products: 35.9 us -> none  [the longest x2 11.8 us: expert_rows(): gate_val = jnp.dot(flat_rows, gate_cols, preferred_element_type=jnp.float32)]
    unnamed x2 -> x16, local copies, waits for them, and re-layouts: 0.01 us -> 23.3 us
    all_to_all x2, blocking collectives: 45.1 us -> 21.9 us  [on_device(): lax.all_to_all(paired, 'expert', split_axis=0, concat_axis=0, tiled=True)]
    pallas_call x0 -> x5, Pallas kernels: none -> 22.7 us  [the longest x2 20.2 us: experts(): pl.pallas_call(experts_kernel, grid=(hidden // block,), in_specs=[whole,...]
    ppermute x0 -> x4, waiting for transfers between devices: none -> 5.41 us  [the longest x2 2.83 us: on_device(): other = lax.ppermute(mine, 'dp', swap)]
    all_gather x2 -> x0, blocking collectives: 4.02 us -> none  [on_device(): paired = lax.all_gather(arrived[:, None], 'dp', axis=1, tiled=True)]
    reduce_sum x6 -> x0, other arithmetic: 1.64 us -> none  [the longest x1 0.87 us: on_device(): jnp.mean(widened * widened, axis=-1, keepdims=True) + 1e-05]
    all_to_all x2, blocking collectives: 26.8 us -> 25.6 us  [on_device(): lax.all_to_all(outgoing, 'expert', split_axis=0, concat_axis=0, tiled=True)]
  transfers between devices with their start and end apart: 0 -> 4, of which waited for: 0 -> 4; matrix products, arithmetic and copies ran while one was open for 0% -> 0% of each run, Pallas kernels for 0% -> 0%
where the time goes in v1:
time: 101 us
  blocking collectives  47.5 us (47%)
  local copies, waits for them, and re-layouts  24.4 us (24%)
  Pallas kernels  22.7 us (22%)
  waiting for transfers between devices  5.41 us (5%)
    all_to_all x2, blocking collectives, on_device(): lax.all_to_all(outgoing, 'expert', split_axis=0, concat_axis=0, tiled=True)  25.6 us
    unnamed x16, local copies, waits for them, and re-layouts  23.3 us
    all_to_all x2, blocking collectives, on_device(): lax.all_to_all(paired, 'expert', split_axis=0, concat_axis=0, tiled=True)  21.9 us
    pallas_call x2, Pallas kernels, experts(): pl.pallas_call(experts_kernel, grid=(hidden // block,), in_specs=[whole,...  20.2 us
    ppermute x2, waiting for transfers between devices, on_device(): other = lax.ppermute(mine, 'dp', swap)  2.83 us
    ppermute x2, waiting for transfers between devices, on_device(): got = lax.ppermute(send, 'dp', swap)  2.58 us
  transfers between devices with their start and end apart: 4, of which 4 were waited for; matrix products, arithmetic and copies ran while one was open for 0% of the time, Pallas kernels for 0%

profile of v1, /device:TPU:0, one launch (start us, length us, event | category | flops | bytes accessed | tf_op | source)
XLA Modules:
  0.0 100.8 jit_solution(8913596722394008600)
XLA Ops:
  0.0 1.5 %first_norm.1 = bf16[4,2880]{1,0:T(4,128)(2,1)} custom-call(bf16[4,2880]{1,0:T(4,128)(2,1)} %state_ref.1, bf16[2,2880]{1,0:T(2,128)(2,1)} %gain_ref.5), custom_call_target="tpu_custom_call" | custom-call | tf_op jit(solution)/shard_map/first_norm/pallas_call | solution.py:24
  1.5 0.8 broadcast_in_dim.4
  2.3 14.9 %all_to_all.20 = bf16[8,4,2880]{2,1,0:T(4,128)(2,1)S(1)} all-to-all(bf16[8,4,2880]{2,1,0:T(4,128)(2,1)S(1)} %broadcast_in_dim.4), channel_id=1, replica_groups=mesh['groups'=2,'expert'=8,'dp'=2] {'expert'}, dimensions={0} | all-to-all | bytes 368640 | tf_op jit(solution)/shard_map/all_to_all | solution.py:126
  17.2 0.1 reshape.14.mine_ref
  17.3 0.1 collective-permute-start
  17.4 1.4 %collective-permute-done.other_ref = bf16[32,2880]{1,0:T(8,128)(2,1)S(1)} collective-permute-done((bf16[32,2880]{1,0:T(8,128)(2,1)S(1)}, bf16[32,2880]{1,0:T(8,128)(2,1)S(1)}, u32[]{:S(2)}, u32[]{:S(2)}) %collective-permute-start) | collective-permute-done | bytes 184352 | tf_op jit(solution)/shard_map/ppermute | solution.py:128
  18.8 0.0 copy-start
  18.8 5.8 %copy-done = bf16[2,2880,1440]{1,2,0:T(8,128)(2,1)S(1)} copy-done((bf16[2,2880,1440]{1,2,0:T(8,128)(2,1)S(1)}, bf16[2,2880,1440]{1,2,0:T(8,128)(2,1)}, u32[]{:S(2)}) %copy-start) | copy-done | bytes 16588824
  24.6 0.0 copy-start.2
  24.6 5.8 %copy-done.2 = bf16[2,2880,1440]{1,2,0:T(8,128)(2,1)S(1)} copy-done((bf16[2,2880,1440]{1,2,0:T(8,128)(2,1)S(1)}, bf16[2,2880,1440]{1,2,0:T(8,128)(2,1)}, u32[]{:S(2)}) %copy-start.2) | copy-done | bytes 16588824
  30.4 0.0 copy-start.4
  30.4 0.0 copy-start.5
  30.4 0.0 copy-start.6
  30.4 0.0 copy-start.7
  30.4 10.2 %experts.2 = (bf16[32,2880]{1,0:T(8,128)(2,1)S(1)}, bf16[32,2880]{1,0:T(8,128)(2,1)S(1)}) custom-call(bf16[32,2880]{1,0:T(8,128)(2,1)S(1)} %reshape.14.mine_ref, bf16[32,2880]{1,0:T(8,128)(2,1)S(1)} %collective-permute-done.other_ref, bf16[2,1440,2880]{2,1,0:T(8,128)(2,1)S(1)} %bitcast.2, bf16[2,1440,2880]{2,1,0:T(8,128)(2,1)S(1)} %bitcast.4, ...), custom_call_target="tpu_custom_call" | custom-call | tf_op jit(solution)/shard_map/experts/pallas_call | solution.py:74
  40.6 0.2 collective-permute-start.1
  40.8 1.3 %collective-permute-done.1 = bf16[32,2880]{1,0:T(8,128)(2,1)S(1)} collective-permute-done((bf16[32,2880]{1,0:T(8,128)(2,1)S(1)}, bf16[32,2880]{1,0:T(8,128)(2,1)S(1)}, u32[]{:S(2)}, u32[]{:S(2)}) %collective-permute-start.1) | collective-permute-done | bytes 184352 | tf_op jit(solution)/shard_map/ppermute | solution.py:130
  42.1 0.1 add.6
  42.1 0.1 reshape.15
  42.2 11.0 %all_to_all.21.parts_ref = bf16[8,4,2880]{2,1,0:T(4,128)(2,1)S(1)} all-to-all(bf16[8,4,2880]{2,1,0:T(4,128)(2,1)S(1)} %reshape.15), channel_id=1, replica_groups=mesh['groups'=2,'expert'=8,'dp'=2] {'expert'}, dimensions={0} | all-to-all | bytes 368640 | tf_op jit(solution)/shard_map/all_to_all | solution.py:132
  53.2 0.0 copy-done.4
  53.2 0.0 copy-done.5
  53.2 0.0 copy-done.6
  53.2 0.0 copy-done.7
  53.2 0.3 combine.2
  53.5 0.1 broadcast_in_dim.5
  53.6 10.6 %all_to_all.22 = bf16[8,4,2880]{2,1,0:T(4,128)(2,1)S(1)} all-to-all(bf16[8,4,2880]{2,1,0:T(4,128)(2,1)S(1)} %broadcast_in_dim.5), channel_id=1, replica_groups=mesh['groups'=2,'expert'=8,'dp'=2] {'expert'}, dimensions={0} | all-to-all | bytes 368640 | tf_op jit(solution)/shard_map/all_to_all | solution.py:126
  64.2 0.1 reshape.16.mine_ref
  64.3 0.1 collective-permute-start.2
  64.4 1.4 %collective-permute-done.2.other_ref = bf16[32,2880]{1,0:T(8,128)(2,1)S(1)} collective-permute-done((bf16[32,2880]{1,0:T(8,128)(2,1)S(1)}, bf16[32,2880]{1,0:T(8,128)(2,1)S(1)}, u32[]{:S(2)}, u32[]{:S(2)}) %collective-permute-start.2) | collective-permute-done | bytes 184352 | tf_op jit(solution)/shard_map/ppermute | solution.py:128
  65.8 0.0 copy-start.1
  65.8 5.8 %copy-done.1 = bf16[2,2880,1440]{1,2,0:T(8,128)(2,1)S(1)} copy-done((bf16[2,2880,1440]{1,2,0:T(8,128)(2,1)S(1)}, bf16[2,2880,1440]{1,2,0:T(8,128)(2,1)}, u32[]{:S(2)}) %copy-start.1) | copy-done | bytes 16588824
  71.6 0.0 copy-start.3
  71.6 5.8 %copy-done.3 = bf16[2,2880,1440]{1,2,0:T(8,128)(2,1)S(1)} copy-done((bf16[2,2880,1440]{1,2,0:T(8,128)(2,1)S(1)}, bf16[2,2880,1440]{1,2,0:T(8,128)(2,1)}, u32[]{:S(2)}) %copy-start.3) | copy-done | bytes 16588824
  77.4 10.1 %experts.3 = (bf16[32,2880]{1,0:T(8,128)(2,1)S(1)}, bf16[32,2880]{1,0:T(8,128)(2,1)S(1)}) custom-call(bf16[32,2880]{1,0:T(8,128)(2,1)S(1)} %reshape.16.mine_ref, bf16[32,2880]{1,0:T(8,128)(2,1)S(1)} %collective-permute-done.2.other_ref, bf16[2,1440,2880]{2,1,0:T(8,128)(2,1)S(1)} %bitcast.3, bf16[2,1440,2880]{2,1,0:T(8,128)(2,1)S(1)} %bitcast.5, ...), custom_call_target="tpu_custom_call" | custom-call | tf_op jit(solution)/shard_map/experts/pallas_call | solution.py:74
  87.5 0.2 collective-permute-start.3
  87.7 1.3 %collective-permute-done.3 = bf16[32,2880]{1,0:T(8,128)(2,1)S(1)} collective-permute-done((bf16[32,2880]{1,0:T(8,128)(2,1)S(1)}, bf16[32,2880]{1,0:T(8,128)(2,1)S(1)}, u32[]{:S(2)}, u32[]{:S(2)}) %collective-permute-start.3) | collective-permute-done | bytes 184352 | tf_op jit(solution)/shard_map/ppermute | solution.py:130
  89.1 0.1 reshape.17
  89.1 10.9 %all_to_all.23.parts_ref = bf16[8,4,2880]{2,1,0:T(4,128)(2,1)S(1)} all-to-all(bf16[8,4,2880]{2,1,0:T(4,128)(2,1)S(1)} %reshape.17), channel_id=1, replica_groups=mesh['groups'=2,'expert'=8,'dp'=2] {'expert'}, dimensions={0} | all-to-all | bytes 368640 | tf_op jit(solution)/shard_map/all_to_all | solution.py:132
  100.0 0.8 combine.3
  (1 shorter events, 0.0 us)
Async XLA Ops:
  17.3 1.5 %collective-permute-start = (bf16[32,2880]{1,0:T(8,128)(2,1)S(1)}, bf16[32,2880]{1,0:T(8,128)(2,1)S(1)}, u32[]{:S(2)}, u32[]{:S(2)}) collective-permute-start(bf16[32,2880]{1,0:T(8,128)(2,1)S(1)} %reshape.14.mine_ref), channel_id=1, source_target_pairs={{0,1},{1,0},{2,3},{3,2},{4,5},{5,4},{6,7},{7,6},{8,9},{9,8},{10,11... | collective-permute-start | bytes 552968 | tf_op jit(solution)/shard_map/ppermute | solution.py:128
  18.8 5.8 %copy-start = (bf16[2,2880,1440]{1,2,0:T(8,128)(2,1)S(1)}, bf16[2,2880,1440]{1,2,0:T(8,128)(2,1)}, u32[]{:S(2)}) copy-start(bf16[2,2880,1440]{1,2,0:T(8,128)(2,1)} %param.9) | copy-start | bytes 49766404
  24.6 5.8 %copy-start.2 = (bf16[2,2880,1440]{1,2,0:T(8,128)(2,1)S(1)}, bf16[2,2880,1440]{1,2,0:T(8,128)(2,1)}, u32[]{:S(2)}) copy-start(bf16[2,2880,1440]{1,2,0:T(8,128)(2,1)} %param.10) | copy-start | bytes 49766404
  30.4 22.8 %copy-start.4 = (bf16[2,2880]{1,0:T(2,128)(2,1)S(1)}, bf16[2,2880]{1,0:T(2,128)(2,1)}, u32[]{:S(2)}) copy-start(bf16[2,2880]{1,0:T(2,128)(2,1)} %gain_ref.5) | copy-start | bytes 34564
  30.4 22.8 %copy-start.5 = (bf16[4,2880]{1,0:T(4,128)(2,1)S(1)}, bf16[4,2880]{1,0:T(4,128)(2,1)}, u32[]{:S(2)}) copy-start(bf16[4,2880]{1,0:T(4,128)(2,1)} %state_ref.1) | copy-start | bytes 69124
  30.4 22.8 %copy-start.6 = (s32[2,4,4]{2,1,0:T(4,128)S(1)}, s32[2,4,4]{2,1,0:T(4,128)}, u32[]{:S(2)}) copy-start(s32[2,4,4]{2,1,0:T(4,128)} %routes_ref.3) | copy-start | bytes 388
  30.4 22.8 %copy-start.7 = (f32[2,4,4]{2,1,0:T(4,128)S(1)}, f32[2,4,4]{2,1,0:T(4,128)}, u32[]{:S(2)}) copy-start(f32[2,4,4]{2,1,0:T(4,128)} %gates_ref.3) | copy-start | bytes 388
  40.6 1.5 %collective-permute-start.1 = (bf16[32,2880]{1,0:T(8,128)(2,1)S(1)}, bf16[32,2880]{1,0:T(8,128)(2,1)S(1)}, u32[]{:S(2)}, u32[]{:S(2)}) collective-permute-start(bf16[32,2880]{1,0:T(8,128)(2,1)S(1)} %get-tuple-element.12), channel_id=1, source_target_pairs={{0,1},{1,0},{2,3},{3,2},{4,5},{5,4},{6,7},{7,6},{8,9},{9,8},{10,11... | collective-permute-start | bytes 552968 | tf_op jit(solution)/shard_map/ppermute | solution.py:130
  64.3 1.5 %collective-permute-start.2 = (bf16[32,2880]{1,0:T(8,128)(2,1)S(1)}, bf16[32,2880]{1,0:T(8,128)(2,1)S(1)}, u32[]{:S(2)}, u32[]{:S(2)}) collective-permute-start(bf16[32,2880]{1,0:T(8,128)(2,1)S(1)} %reshape.16.mine_ref), channel_id=1, source_target_pairs={{0,1},{1,0},{2,3},{3,2},{4,5},{5,4},{6,7},{7,6},{8,9},{9,8},{10,11... | collective-permute-start | bytes 552968 | tf_op jit(solution)/shard_map/ppermute | solution.py:128
  65.8 5.8 %copy-start.1 = (bf16[2,2880,1440]{1,2,0:T(8,128)(2,1)S(1)}, bf16[2,2880,1440]{1,2,0:T(8,128)(2,1)}, u32[]{:S(2)}) copy-start(bf16[2,2880,1440]{1,2,0:T(8,128)(2,1)} %param.9) | copy-start | bytes 49766404
  71.6 5.8 %copy-start.3 = (bf16[2,2880,1440]{1,2,0:T(8,128)(2,1)S(1)}, bf16[2,2880,1440]{1,2,0:T(8,128)(2,1)}, u32[]{:S(2)}) copy-start(bf16[2,2880,1440]{1,2,0:T(8,128)(2,1)} %param.10) | copy-start | bytes 49766404
  87.5 1.5 %collective-permute-start.3 = (bf16[32,2880]{1,0:T(8,128)(2,1)S(1)}, bf16[32,2880]{1,0:T(8,128)(2,1)S(1)}, u32[]{:S(2)}, u32[]{:S(2)}) collective-permute-start(bf16[32,2880]{1,0:T(8,128)(2,1)S(1)} %get-tuple-element.16), channel_id=1, source_target_pairs={{0,1},{1,0},{2,3},{3,2},{4,5},{5,4},{6,7},{7,6},{8,9},{9,8},{10,11... | collective-permute-start | bytes 552968 | tf_op jit(solution)/shard_map/ppermute | solution.py:130

commit v2 on v1

--- a/solution.py
+++ b/solution.py
@@ -8,7 +8,7 @@
 from jax.sharding import PartitionSpec as P
 
 EPS = 1e-05
-VMEM_LIMIT = 20 * 1024 * 1024
+VMEM_LIMIT = 50 * 1024 * 1024
 
 
 def normalise(value, gain_row):
@@ -69,7 +69,7 @@
     half, width = mine.shape
     hidden = down_rows.shape[1]
     block = hidden_block(hidden)
-    whole = pl.BlockSpec((half, width), lambda i: (0, 0))
+    whole = pl.BlockSpec(memory_space=pltpu.VMEM)
     weight = pl.BlockSpec((1, block, width), lambda i: (layer_idx, i, 0))
     return pl.pallas_call(
         experts_kernel,
@@ -104,7 +104,6 @@
     return pl.pallas_call(
         functools.partial(combine_kernel, layer_idx, chips_per_expert, last),
         out_shape=[shape] if last else [shape, shape],
-        compiler_params=pltpu.CompilerParams(vmem_limit_bytes=VMEM_LIMIT),
         name="combine",
     )(state, parts, routes, gates, norm_gain)
 

time: 101 us -> 87.5 us (0.87)
  local copies, waits for them, and re-layouts: 24.4 us -> 1.84 us
  Pallas kernels: 22.7 us -> 30.5 us
    unnamed x16 -> x0, local copies, waits for them, and re-layouts: 23.3 us -> none
    pallas_call x2, Pallas kernels: 20.2 us -> 25.5 us  [experts(): pl.pallas_call(experts_kernel, grid=(hidden // block,), in_specs=[whole,...]
    pallas_call x2, Pallas kernels: 1.02 us -> 3.48 us  [combine(): pl.pallas_call(functools.partial(combine_kernel, layer_idx, chips_per_exp...]
    all_to_all x2, blocking collectives: 21.9 us -> 23 us  [on_device(): lax.all_to_all(paired, 'expert', split_axis=0, concat_axis=0, tiled=True)]
where the time goes in v2:
time: 87.5 us; the launch traced here: 87 us
  blocking collectives  48.5 us (55%)
  Pallas kernels  30.5 us (35%)
  waiting for transfers between devices  5.41 us (6%)
  local copies, waits for them, and re-layouts  1.84 us (2%)
    all_to_all x2, blocking collectives, on_device(): lax.all_to_all(outgoing, 'expert', split_axis=0, concat_axis=0, tiled=True)  25.5 us
    pallas_call x2, Pallas kernels, experts(): pl.pallas_call(experts_kernel, grid=(hidden // block,), in_specs=[whole,...  25.5 us
    all_to_all x2, blocking collectives, on_device(): lax.all_to_all(paired, 'expert', split_axis=0, concat_axis=0, tiled=True)  23 us
    pallas_call x2, Pallas kernels, combine(): pl.pallas_call(functools.partial(combine_kernel, layer_idx, chips_per_exp...  3.48 us
    ppermute x2, waiting for transfers between devices, on_device(): other = lax.ppermute(mine, 'dp', swap)  2.83 us
    ppermute x2, waiting for transfers between devices, on_device(): got = lax.ppermute(send, 'dp', swap)  2.58 us
  transfers between devices with their start and end apart: 4, of which 4 were waited for; matrix products, arithmetic and copies ran while one was open for 0% of the time, Pallas kernels for 0%

profile of v2, /device:TPU:0, one launch (start us, length us, event | category | flops | bytes accessed | tf_op | source)
XLA Modules:
  0.0 87.0 jit_solution(10926813861007182187)
XLA Ops:
  0.0 1.5 %first_norm.1 = bf16[4,2880]{1,0:T(4,128)(2,1)} custom-call(bf16[4,2880]{1,0:T(4,128)(2,1)} %state_ref.1, bf16[2,2880]{1,0:T(2,128)(2,1)} %gain_ref.5), custom_call_target="tpu_custom_call" | custom-call | tf_op jit(solution)/shard_map/first_norm/pallas_call | solution.py:24
  1.5 0.8 broadcast_in_dim.4
  2.3 14.9 %all_to_all.20 = bf16[8,4,2880]{2,1,0:T(4,128)(2,1)S(1)} all-to-all(bf16[8,4,2880]{2,1,0:T(4,128)(2,1)S(1)} %broadcast_in_dim.4), channel_id=1, replica_groups=mesh['groups'=2,'expert'=8,'dp'=2] {'expert'}, dimensions={0} | all-to-all | bytes 368640 | tf_op jit(solution)/shard_map/all_to_all | solution.py:125
  17.2 0.1 reshape.14.mine_ref
  17.3 0.1 collective-permute-start
  17.4 1.4 %collective-permute-done.other_ref = bf16[32,2880]{1,0:T(8,128)(2,1)S(1)} collective-permute-done((bf16[32,2880]{1,0:T(8,128)(2,1)S(1)}, bf16[32,2880]{1,0:T(8,128)(2,1)S(1)}, u32[]{:S(2)}, u32[]{:S(2)}) %collective-permute-start) | collective-permute-done | bytes 184352 | tf_op jit(solution)/shard_map/ppermute | solution.py:127
  18.8 12.7 %experts.2 = (bf16[32,2880]{1,0:T(8,128)(2,1)S(1)}, bf16[32,2880]{1,0:T(8,128)(2,1)S(1)}) custom-call(bf16[32,2880]{1,0:T(8,128)(2,1)S(1)} %reshape.14.mine_ref, bf16[32,2880]{1,0:T(8,128)(2,1)S(1)} %collective-permute-done.other_ref, bf16[2,1440,2880]{2,1,0:T(8,128)(2,1)} %bitcast.2, bf16[2,1440,2880]{2,1,0:T(8,128)(2,1)} %bitcast.4, ...), custom_call_target="tpu_custom_call" | custom-call | tf_op jit(solution)/shard_map/experts/pallas_call | solution.py:74
  31.5 0.2 collective-permute-start.1
  31.7 1.3 %collective-permute-done.1 = bf16[32,2880]{1,0:T(8,128)(2,1)S(1)} collective-permute-done((bf16[32,2880]{1,0:T(8,128)(2,1)S(1)}, bf16[32,2880]{1,0:T(8,128)(2,1)S(1)}, u32[]{:S(2)}, u32[]{:S(2)}) %collective-permute-start.1) | collective-permute-done | bytes 184352 | tf_op jit(solution)/shard_map/ppermute | solution.py:129
  33.0 0.1 add.6
  33.1 0.1 reshape.15
  33.1 11.5 %all_to_all.21.parts_ref = bf16[8,4,2880]{2,1,0:T(4,128)(2,1)} all-to-all(bf16[8,4,2880]{2,1,0:T(4,128)(2,1)S(1)} %reshape.15), channel_id=1, replica_groups=mesh['groups'=2,'expert'=8,'dp'=2] {'expert'}, dimensions={0} | all-to-all | bytes 368640 | tf_op jit(solution)/shard_map/all_to_all | solution.py:131
  44.6 1.8 %combine.2 = (bf16[4,2880]{1,0:T(4,128)(2,1)}, bf16[4,2880]{1,0:T(4,128)(2,1)}) custom-call(bf16[4,2880]{1,0:T(4,128)(2,1)} %state_ref.1, bf16[8,4,2880]{2,1,0:T(4,128)(2,1)} %all_to_all.21.parts_ref, s32[2,4,4]{2,1,0:T(4,128)} %routes_ref.3, f32[2,4,4]{2,1,0:T(4,128)} %gates_ref.3, bf16[2,2880]{1,0:T(2,128)(2,1)} %gain_ref.5), custom_call_target="tpu_custom_call" | custom-call | tf_op jit(solution)/shard_map/combine/pallas_call | solution.py:104
  46.4 0.8 broadcast_in_dim.5
  47.2 10.6 %all_to_all.22 = bf16[8,4,2880]{2,1,0:T(4,128)(2,1)S(1)} all-to-all(bf16[8,4,2880]{2,1,0:T(4,128)(2,1)S(1)} %broadcast_in_dim.5), channel_id=1, replica_groups=mesh['groups'=2,'expert'=8,'dp'=2] {'expert'}, dimensions={0} | all-to-all | bytes 368640 | tf_op jit(solution)/shard_map/all_to_all | solution.py:125
  57.8 0.1 reshape.16.mine_ref
  57.9 0.1 collective-permute-start.2
  58.0 1.4 %collective-permute-done.2.other_ref = bf16[32,2880]{1,0:T(8,128)(2,1)S(1)} collective-permute-done((bf16[32,2880]{1,0:T(8,128)(2,1)S(1)}, bf16[32,2880]{1,0:T(8,128)(2,1)S(1)}, u32[]{:S(2)}, u32[]{:S(2)}) %collective-permute-start.2) | collective-permute-done | bytes 184352 | tf_op jit(solution)/shard_map/ppermute | solution.py:127
  59.4 12.8 %experts.3 = (bf16[32,2880]{1,0:T(8,128)(2,1)S(1)}, bf16[32,2880]{1,0:T(8,128)(2,1)S(1)}) custom-call(bf16[32,2880]{1,0:T(8,128)(2,1)S(1)} %reshape.16.mine_ref, bf16[32,2880]{1,0:T(8,128)(2,1)S(1)} %collective-permute-done.2.other_ref, bf16[2,1440,2880]{2,1,0:T(8,128)(2,1)} %bitcast.3, bf16[2,1440,2880]{2,1,0:T(8,128)(2,1)} %bitcast.5, ...), custom_call_target="tpu_custom_call" | custom-call | tf_op jit(solution)/shard_map/experts/pallas_call | solution.py:74
  72.2 0.2 collective-permute-start.3
  72.4 1.3 %collective-permute-done.3 = bf16[32,2880]{1,0:T(8,128)(2,1)S(1)} collective-permute-done((bf16[32,2880]{1,0:T(8,128)(2,1)S(1)}, bf16[32,2880]{1,0:T(8,128)(2,1)S(1)}, u32[]{:S(2)}, u32[]{:S(2)}) %collective-permute-start.3) | collective-permute-done | bytes 184352 | tf_op jit(solution)/shard_map/ppermute | solution.py:129
  73.7 0.1 reshape.17
  73.8 11.5 %all_to_all.23.parts_ref = bf16[8,4,2880]{2,1,0:T(4,128)(2,1)} all-to-all(bf16[8,4,2880]{2,1,0:T(4,128)(2,1)S(1)} %reshape.17), channel_id=1, replica_groups=mesh['groups'=2,'expert'=8,'dp'=2] {'expert'}, dimensions={0} | all-to-all | bytes 368640 | tf_op jit(solution)/shard_map/all_to_all | solution.py:131
  85.3 1.7 %combine.3 = bf16[4,2880]{1,0:T(4,128)(2,1)} custom-call(bf16[4,2880]{1,0:T(4,128)(2,1)} %get-tuple-element.13.state_ref, bf16[8,4,2880]{2,1,0:T(4,128)(2,1)} %all_to_all.23.parts_ref, s32[2,4,4]{2,1,0:T(4,128)} %routes_ref.3, f32[2,4,4]{2,1,0:T(4,128)} %gates_ref.3, bf16[2,2880]{1,0:T(2,128)(2,1)} %gain_ref.5), custom_call_target="tpu_custom_call" | custom-call | tf_op jit(solution)/shard_map/combine/pallas_call | solution.py:104
  (1 shorter events, 0.0 us)
Async XLA Ops:
  17.3 1.5 %collective-permute-start = (bf16[32,2880]{1,0:T(8,128)(2,1)S(1)}, bf16[32,2880]{1,0:T(8,128)(2,1)S(1)}, u32[]{:S(2)}, u32[]{:S(2)}) collective-permute-start(bf16[32,2880]{1,0:T(8,128)(2,1)S(1)} %reshape.14.mine_ref), channel_id=1, source_target_pairs={{0,1},{1,0},{2,3},{3,2},{4,5},{5,4},{6,7},{7,6},{8,9},{9,8},{10,11... | collective-permute-start | bytes 552968 | tf_op jit(solution)/shard_map/ppermute | solution.py:127
  31.5 1.5 %collective-permute-start.1 = (bf16[32,2880]{1,0:T(8,128)(2,1)S(1)}, bf16[32,2880]{1,0:T(8,128)(2,1)S(1)}, u32[]{:S(2)}, u32[]{:S(2)}) collective-permute-start(bf16[32,2880]{1,0:T(8,128)(2,1)S(1)} %get-tuple-element.12), channel_id=1, source_target_pairs={{0,1},{1,0},{2,3},{3,2},{4,5},{5,4},{6,7},{7,6},{8,9},{9,8},{10,11... | collective-permute-start | bytes 552968 | tf_op jit(solution)/shard_map/ppermute | solution.py:129
  57.9 1.5 %collective-permute-start.2 = (bf16[32,2880]{1,0:T(8,128)(2,1)S(1)}, bf16[32,2880]{1,0:T(8,128)(2,1)S(1)}, u32[]{:S(2)}, u32[]{:S(2)}) collective-permute-start(bf16[32,2880]{1,0:T(8,128)(2,1)S(1)} %reshape.16.mine_ref), channel_id=1, source_target_pairs={{0,1},{1,0},{2,3},{3,2},{4,5},{5,4},{6,7},{7,6},{8,9},{9,8},{10,11... | collective-permute-start | bytes 552968 | tf_op jit(solution)/shard_map/ppermute | solution.py:127
  72.2 1.5 %collective-permute-start.3 = (bf16[32,2880]{1,0:T(8,128)(2,1)S(1)}, bf16[32,2880]{1,0:T(8,128)(2,1)S(1)}, u32[]{:S(2)}, u32[]{:S(2)}) collective-permute-start(bf16[32,2880]{1,0:T(8,128)(2,1)S(1)} %get-tuple-element.16), channel_id=1, source_target_pairs={{0,1},{1,0},{2,3},{3,2},{4,5},{5,4},{6,7},{7,6},{8,9},{9,8},{10,11... | collective-permute-start | bytes 552968 | tf_op jit(solution)/shard_map/ppermute | solution.py:129

commit v3 on v2

--- a/solution.py
+++ b/solution.py
@@ -23,13 +23,15 @@
 def first_norm(tokens, norm_gain):
     return pl.pallas_call(
         first_norm_kernel,
+        in_specs=[pl.BlockSpec(memory_space=pltpu.VMEM)] * 2,
+        out_specs=pl.BlockSpec(memory_space=pltpu.VMEM),
         out_shape=jax.ShapeDtypeStruct(tokens.shape, jnp.bfloat16),
         name="first_norm",
     )(tokens, norm_gain)
 
 
 def hidden_block(hidden):
-    for block in (240, 480, 288, 144, 96, 720):
+    for block in (480, 240, 288, 144, 96):
         if hidden % block == 0:
             return block
     return hidden
@@ -101,8 +103,11 @@
 
 def combine(layer_idx, last, chips_per_expert, state, parts, routes, gates, norm_gain):
     shape = jax.ShapeDtypeStruct(state.shape, jnp.bfloat16)
+    whole = pl.BlockSpec(memory_space=pltpu.VMEM)
     return pl.pallas_call(
         functools.partial(combine_kernel, layer_idx, chips_per_expert, last),
+        in_specs=[whole] * 5,
+        out_specs=[whole] if last else [whole, whole],
         out_shape=[shape] if last else [shape, shape],
         name="combine",
     )(state, parts, routes, gates, norm_gain)

time: 87.5 us -> 85.5 us (0.977)
  Pallas kernels: 30.5 us -> 28.5 us
    pallas_call x2, Pallas kernels: 25.5 us -> 23.5 us  [experts(): pl.pallas_call(experts_kernel, grid=(hidden // block,), in_specs=[whole,...]
where the time goes in v3:
time: 85.5 us; the launch traced here: 85 us
  blocking collectives  48.5 us (57%)
  Pallas kernels  28.5 us (33%)
  waiting for transfers between devices  5.4 us (6%)
  local copies, waits for them, and re-layouts  1.84 us (2%)
    all_to_all x2, blocking collectives, on_device(): lax.all_to_all(outgoing, 'expert', split_axis=0, concat_axis=0, tiled=True)  25.5 us
    pallas_call x2, Pallas kernels, experts(): pl.pallas_call(experts_kernel, grid=(hidden // block,), in_specs=[whole,...  23.5 us
    all_to_all x2, blocking collectives, on_device(): lax.all_to_all(paired, 'expert', split_axis=0, concat_axis=0, tiled=True)  23 us
    pallas_call x2, Pallas kernels, combine(): pl.pallas_call(functools.partial(combine_kernel, layer_idx, chips_per_exp...  3.48 us
    ppermute x2, waiting for transfers between devices, on_device(): other = lax.ppermute(mine, 'dp', swap)  2.83 us
    ppermute x2, waiting for transfers between devices, on_device(): got = lax.ppermute(send, 'dp', swap)  2.57 us
  transfers between devices with their start and end apart: 4, of which 4 were waited for; matrix products, arithmetic and copies ran while one was open for 0% of the time, Pallas kernels for 0%

profile of v3, /device:TPU:0, one launch (start us, length us, event | category | flops | bytes accessed | tf_op | source)
XLA Modules:
  0.0 85.0 jit_solution(856375077470670301)
XLA Ops:
  0.0 1.5 %first_norm.1 = bf16[4,2880]{1,0:T(4,128)(2,1)} custom-call(bf16[4,2880]{1,0:T(4,128)(2,1)} %state_ref.1, bf16[2,2880]{1,0:T(2,128)(2,1)} %gain_ref.5), custom_call_target="tpu_custom_call" | custom-call | tf_op jit(solution)/shard_map/first_norm/pallas_call | solution.py:24
  1.5 0.8 broadcast_in_dim.4
  2.3 14.9 %all_to_all.20 = bf16[8,4,2880]{2,1,0:T(4,128)(2,1)S(1)} all-to-all(bf16[8,4,2880]{2,1,0:T(4,128)(2,1)S(1)} %broadcast_in_dim.4), channel_id=1, replica_groups=mesh['groups'=2,'expert'=8,'dp'=2] {'expert'}, dimensions={0} | all-to-all | bytes 368640 | tf_op jit(solution)/shard_map/all_to_all | solution.py:130
  17.2 0.1 reshape.14.mine_ref
  17.3 0.1 collective-permute-start
  17.4 1.4 %collective-permute-done.other_ref = bf16[32,2880]{1,0:T(8,128)(2,1)S(1)} collective-permute-done((bf16[32,2880]{1,0:T(8,128)(2,1)S(1)}, bf16[32,2880]{1,0:T(8,128)(2,1)S(1)}, u32[]{:S(2)}, u32[]{:S(2)}) %collective-permute-start) | collective-permute-done | bytes 184352 | tf_op jit(solution)/shard_map/ppermute | solution.py:132
  18.8 11.8 %experts.2 = (bf16[32,2880]{1,0:T(8,128)(2,1)S(1)}, bf16[32,2880]{1,0:T(8,128)(2,1)S(1)}) custom-call(bf16[32,2880]{1,0:T(8,128)(2,1)S(1)} %reshape.14.mine_ref, bf16[32,2880]{1,0:T(8,128)(2,1)S(1)} %collective-permute-done.other_ref, bf16[2,1440,2880]{2,1,0:T(8,128)(2,1)} %bitcast.2, bf16[2,1440,2880]{2,1,0:T(8,128)(2,1)} %bitcast.4, ...), custom_call_target="tpu_custom_call" | custom-call | tf_op jit(solution)/shard_map/experts/pallas_call | solution.py:76
  30.5 0.2 collective-permute-start.1
  30.7 1.3 %collective-permute-done.1 = bf16[32,2880]{1,0:T(8,128)(2,1)S(1)} collective-permute-done((bf16[32,2880]{1,0:T(8,128)(2,1)S(1)}, bf16[32,2880]{1,0:T(8,128)(2,1)S(1)}, u32[]{:S(2)}, u32[]{:S(2)}) %collective-permute-start.1) | collective-permute-done | bytes 184352 | tf_op jit(solution)/shard_map/ppermute | solution.py:134
  32.0 0.1 add.6
  32.1 0.1 reshape.15
  32.1 11.5 %all_to_all.21.parts_ref = bf16[8,4,2880]{2,1,0:T(4,128)(2,1)} all-to-all(bf16[8,4,2880]{2,1,0:T(4,128)(2,1)S(1)} %reshape.15), channel_id=1, replica_groups=mesh['groups'=2,'expert'=8,'dp'=2] {'expert'}, dimensions={0} | all-to-all | bytes 368640 | tf_op jit(solution)/shard_map/all_to_all | solution.py:136
  43.6 1.8 %combine.2 = (bf16[4,2880]{1,0:T(4,128)(2,1)}, bf16[4,2880]{1,0:T(4,128)(2,1)}) custom-call(bf16[4,2880]{1,0:T(4,128)(2,1)} %state_ref.1, bf16[8,4,2880]{2,1,0:T(4,128)(2,1)} %all_to_all.21.parts_ref, s32[2,4,4]{2,1,0:T(4,128)} %routes_ref.3, f32[2,4,4]{2,1,0:T(4,128)} %gates_ref.3, bf16[2,2880]{1,0:T(2,128)(2,1)} %gain_ref.5), custom_call_target="tpu_custom_call" | custom-call | tf_op jit(solution)/shard_map/combine/pallas_call | solution.py:107
  45.4 0.8 broadcast_in_dim.5
  46.2 10.6 %all_to_all.22 = bf16[8,4,2880]{2,1,0:T(4,128)(2,1)S(1)} all-to-all(bf16[8,4,2880]{2,1,0:T(4,128)(2,1)S(1)} %broadcast_in_dim.5), channel_id=1, replica_groups=mesh['groups'=2,'expert'=8,'dp'=2] {'expert'}, dimensions={0} | all-to-all | bytes 368640 | tf_op jit(solution)/shard_map/all_to_all | solution.py:130
  56.8 0.1 reshape.16.mine_ref
  56.9 0.1 collective-permute-start.2
  57.0 1.4 %collective-permute-done.2.other_ref = bf16[32,2880]{1,0:T(8,128)(2,1)S(1)} collective-permute-done((bf16[32,2880]{1,0:T(8,128)(2,1)S(1)}, bf16[32,2880]{1,0:T(8,128)(2,1)S(1)}, u32[]{:S(2)}, u32[]{:S(2)}) %collective-permute-start.2) | collective-permute-done | bytes 184352 | tf_op jit(solution)/shard_map/ppermute | solution.py:132
  58.4 11.8 %experts.3 = (bf16[32,2880]{1,0:T(8,128)(2,1)S(1)}, bf16[32,2880]{1,0:T(8,128)(2,1)S(1)}) custom-call(bf16[32,2880]{1,0:T(8,128)(2,1)S(1)} %reshape.16.mine_ref, bf16[32,2880]{1,0:T(8,128)(2,1)S(1)} %collective-permute-done.2.other_ref, bf16[2,1440,2880]{2,1,0:T(8,128)(2,1)} %bitcast.3, bf16[2,1440,2880]{2,1,0:T(8,128)(2,1)} %bitcast.5, ...), custom_call_target="tpu_custom_call" | custom-call | tf_op jit(solution)/shard_map/experts/pallas_call | solution.py:76
  70.2 0.2 collective-permute-start.3
  70.4 1.3 %collective-permute-done.3 = bf16[32,2880]{1,0:T(8,128)(2,1)S(1)} collective-permute-done((bf16[32,2880]{1,0:T(8,128)(2,1)S(1)}, bf16[32,2880]{1,0:T(8,128)(2,1)S(1)}, u32[]{:S(2)}, u32[]{:S(2)}) %collective-permute-start.3) | collective-permute-done | bytes 184352 | tf_op jit(solution)/shard_map/ppermute | solution.py:134
  71.7 0.1 reshape.17
  71.8 11.5 %all_to_all.23.parts_ref = bf16[8,4,2880]{2,1,0:T(4,128)(2,1)} all-to-all(bf16[8,4,2880]{2,1,0:T(4,128)(2,1)S(1)} %reshape.17), channel_id=1, replica_groups=mesh['groups'=2,'expert'=8,'dp'=2] {'expert'}, dimensions={0} | all-to-all | bytes 368640 | tf_op jit(solution)/shard_map/all_to_all | solution.py:136
  83.3 1.7 %combine.3 = bf16[4,2880]{1,0:T(4,128)(2,1)} custom-call(bf16[4,2880]{1,0:T(4,128)(2,1)} %get-tuple-element.13.state_ref, bf16[8,4,2880]{2,1,0:T(4,128)(2,1)} %all_to_all.23.parts_ref, s32[2,4,4]{2,1,0:T(4,128)} %routes_ref.3, f32[2,4,4]{2,1,0:T(4,128)} %gates_ref.3, bf16[2,2880]{1,0:T(2,128)(2,1)} %gain_ref.5), custom_call_target="tpu_custom_call" | custom-call | tf_op jit(solution)/shard_map/combine/pallas_call | solution.py:107
  (1 shorter events, 0.0 us)
Async XLA Ops:
  17.3 1.5 %collective-permute-start = (bf16[32,2880]{1,0:T(8,128)(2,1)S(1)}, bf16[32,2880]{1,0:T(8,128)(2,1)S(1)}, u32[]{:S(2)}, u32[]{:S(2)}) collective-permute-start(bf16[32,2880]{1,0:T(8,128)(2,1)S(1)} %reshape.14.mine_ref), channel_id=1, source_target_pairs={{0,1},{1,0},{2,3},{3,2},{4,5},{5,4},{6,7},{7,6},{8,9},{9,8},{10,11... | collective-permute-start | bytes 552968 | tf_op jit(solution)/shard_map/ppermute | solution.py:132
  30.5 1.5 %collective-permute-start.1 = (bf16[32,2880]{1,0:T(8,128)(2,1)S(1)}, bf16[32,2880]{1,0:T(8,128)(2,1)S(1)}, u32[]{:S(2)}, u32[]{:S(2)}) collective-permute-start(bf16[32,2880]{1,0:T(8,128)(2,1)S(1)} %get-tuple-element.12), channel_id=1, source_target_pairs={{0,1},{1,0},{2,3},{3,2},{4,5},{5,4},{6,7},{7,6},{8,9},{9,8},{10,11... | collective-permute-start | bytes 552968 | tf_op jit(solution)/shard_map/ppermute | solution.py:134
  56.9 1.5 %collective-permute-start.2 = (bf16[32,2880]{1,0:T(8,128)(2,1)S(1)}, bf16[32,2880]{1,0:T(8,128)(2,1)S(1)}, u32[]{:S(2)}, u32[]{:S(2)}) collective-permute-start(bf16[32,2880]{1,0:T(8,128)(2,1)S(1)} %reshape.16.mine_ref), channel_id=1, source_target_pairs={{0,1},{1,0},{2,3},{3,2},{4,5},{5,4},{6,7},{7,6},{8,9},{9,8},{10,11... | collective-permute-start | bytes 552968 | tf_op jit(solution)/shard_map/ppermute | solution.py:132
  70.2 1.5 %collective-permute-start.3 = (bf16[32,2880]{1,0:T(8,128)(2,1)S(1)}, bf16[32,2880]{1,0:T(8,128)(2,1)S(1)}, u32[]{:S(2)}, u32[]{:S(2)}) collective-permute-start(bf16[32,2880]{1,0:T(8,128)(2,1)S(1)} %get-tuple-element.16), channel_id=1, source_target_pairs={{0,1},{1,0},{2,3},{3,2},{4,5},{5,4},{6,7},{7,6},{8,9},{9,8},{10,11... | collective-permute-start | bytes 552968 | tf_op jit(solution)/shard_map/ppermute | solution.py:134
